TPU v7x, 32 devices: a whole 2x2x4 slice. The times are simulated.
32 devices in a mesh: ad: 8 (over z, y), tp: 4 (over x, core).
Axes of the slice: x: 2, y: 2, z: 4, core: 2. Of those that a mesh axis runs over, the one named last changes fastest.
Arguments:
- hidden: bfloat16 [256, 8192], P('ad', 'tp'), may hold values from -6 to 6
- queries: bfloat16 [256, 64, 128], P('ad', 'tp'), may hold values from -170 to 170
- key_cache_rows: bfloat16 [256, 8, 128, 128], P('ad', 'tp'), may hold values from -6 to 6
- value_cache_rows: bfloat16 [256, 8, 128, 128], P('ad', 'tp'), may hold values from -6 to 6
- cache_fill_length: int32 [256], P('ad'), may hold values from 1 to 128, as said below
- adapter_choice_index: int32 [256], P('ad'), may hold values from 0 to 511, as said below
- key_value_weight: bfloat16 [8192, 2, 1024], P(None, None, 'tp'), may hold values from -0.0625 to 0.0625
- adapter_down_weight: bfloat16 [512, 16, 8192], P('ad', None, 'tp'), may hold values from -0.0625 to 0.0625
- adapter_up_weight: bfloat16 [512, 16, 2, 1024], P('ad', None, None, 'tp'), may hold values from -1.5 to 1.5
Outputs:
- appended_entries: bfloat16 [256, 2, 8, 128], P('ad', None, 'tp')
- context: bfloat16 [256, 64, 128], P('ad', 'tp')
Inputs may be any that keep to these rules, and one draw needn't show every extreme that they name: `adapter_choice_index`: adapter a is held by index a // 64 of ad. Among the 32 sequences of one index of ad, at most 4 name adapters of one holder; in every draw one holder receives exactly 4 from every index of ad. `cache_fill_length`: in every block of 32 sequences one has 128.
All inputs are finite; a program needn't handle non-finite values.
Results may differ from a plain program's by a relative error of at most 0.0053.
Values may be sent and summed in bfloat16 or wider, within the bound.
A program may use at most 128 MiB of HBM per device.

v0:
```python
import functools

import jax
import jax.numpy as jnp
from jax import lax
from jax.experimental import pallas as pl
from jax.experimental.pallas import tpu as pltpu
from jax.sharding import PartitionSpec as P

MODEL_WIDTH = 8192
CAP = 4
adapter_scale = 0.5
epsilon = 1e-05
LANES = 128
MESH = pl.DeviceIdType.MESH
F32 = jnp.float32
BF16 = jnp.bfloat16


def iota(shape, dim):
    return lax.broadcasted_iota(jnp.int32, shape, dim)


def dot_last(a, b):
    return lax.dot_general(a, b, (((1,), (1,)), ((), ())), preferred_element_type=F32)


def kernel(
    n_ad, n_tp, rank, idx_ref, fill_ref, hid_in, q_in, k_in, v_in, w_in, dn_in, up_in,
    app_ref, ctx_ref,
    h_all, q_s, k_s, v_s, w_s, dn_s, up_s,
    sb, rb, pb, db, ret, lhs_s, acc_s, m_s, l_s,
    in_sem, w_sem, up_sem, own_sem,
    slab_send, slab_recv, row_send, row_recv, lat_send, lat_recv, ret_send, ret_recv,
):
    ad = lax.axis_index("ad")
    tp = lax.axis_index("tp")
    rows, slab = hid_in.shape
    half = slab // 2
    pack_rows = n_ad * 2 * CAP
    adapters = dn_in.shape[0] // rank
    per = LANES // rank
    groups = adapters // per
    width = w_in.shape[2]
    tiles = width // LANES
    head = q_in.shape[2]
    heads = q_in.shape[1]
    kv = k_in.shape[1]
    group = heads // kv
    ctx = k_in.shape[2]
    scale = head ** (-0.5)

    hid_copy = pltpu.make_async_copy(hid_in, h_all.at[tp], in_sem.at[0])
    q_copy = pltpu.make_async_copy(q_in, q_s, in_sem.at[1])
    k_copy = pltpu.make_async_copy(k_in, k_s, in_sem.at[2])
    v_copy = pltpu.make_async_copy(v_in, v_s, in_sem.at[3])
    dn_copy = pltpu.make_async_copy(dn_in, dn_s, in_sem.at[4])
    up_copies = [
        pltpu.make_async_copy(up_in.at[:, :, pl.ds(c * LANES, LANES)], up_s.at[c], up_sem.at[c])
        for c in range(tiles)
    ]
    w_copies = [
        pltpu.make_async_copy(
            w_in.at[pl.ds(i * slab, slab), :, pl.ds(c * LANES, LANES)],
            w_s.at[c, pl.ds(i * slab, slab)],
            w_sem.at[i * tiles + c],
        )
        for i in range(n_tp)
        for c in range(tiles)
    ]
    for c in (hid_copy, q_copy, k_copy, v_copy, dn_copy, *up_copies, *w_copies):
        c.start()

    ad_peers = [lax.rem(ad + i, n_ad) for i in range(1, n_ad)]
    tp_peers = [lax.rem(tp + i, n_tp) for i in range(1, n_tp)]
    far = lax.rem(tp + 2, n_tp)
    near = tp + 1 - 2 * lax.rem(tp, 2)

    barrier = pltpu.get_barrier_semaphore()
    for o in ad_peers:
        pl.semaphore_signal(barrier, inc=1, device_id=(o, tp), device_id_type=MESH)
    for t in tp_peers:
        pl.semaphore_signal(barrier, inc=1, device_id=(ad, t), device_id_type=MESH)

    parity = jnp.concatenate(
        [
            jnp.where(
                iota((LANES, 2 * LANES), 1) == 2 * iota((LANES, 2 * LANES), 0) + kind, 1.0, 0.0
            ).astype(BF16)
            for kind in range(2)
        ],
        axis=1,
    )

    idx_r = jnp.broadcast_to(idx_ref[...].astype(F32), (rows, rows))
    eye = iota((rows, rows), 0) == iota((rows, rows), 1)
    idx_c = jnp.sum(jnp.where(eye, idx_r, 0.0), axis=1, keepdims=True)
    owner_r = jnp.zeros((rows, rows), F32)
    owner_c = jnp.zeros((rows, 1), F32)
    for o in range(1, n_ad):
        owner_r = owner_r + jnp.where(idx_r >= o * adapters, 1.0, 0.0)
        owner_c = owner_c + jnp.where(idx_c >= o * adapters, 1.0, 0.0)
    local_r = idx_r - owner_r * adapters
    same = owner_r == owner_c
    before = iota((rows, rows), 1) < iota((rows, rows), 0)
    after = iota((rows, rows), 0) < iota((rows, rows), 1)
    place_c = jnp.sum(jnp.where(same & before, 1.0, 0.0), axis=1, keepdims=True)
    place_r = jnp.sum(jnp.where(same & after, 1.0, 0.0), axis=0, keepdims=True)
    target_r = owner_r[0:1] * (2 * CAP) + place_r
    target_c = owner_c * (2 * CAP) + place_c
    row_id = iota((pack_rows, rows), 0).astype(F32)
    low = jnp.where(row_id == target_r, 1.0, 0.0)
    high = jnp.where(row_id == target_r + CAP, 1.0, 0.0)
    both = low + high
    ids_out = jnp.sum(both * local_r[0:1], axis=1, keepdims=True) + adapters * (
        1.0 - jnp.sum(both, axis=1, keepdims=True)
    )

    hid_copy.wait()
    mine = h_all[tp]
    packed = jnp.dot(low.astype(BF16), mine[:, :half], preferred_element_type=F32) + jnp.dot(
        high.astype(BF16), mine[:, half:], preferred_element_type=F32
    )
    sb[:, :, 0:half] = packed.reshape(n_ad, 2 * CAP, half).astype(BF16)
    sb[:, :, half : half + LANES] = (
        jnp.broadcast_to(ids_out, (pack_rows, LANES)).reshape(n_ad, 2 * CAP, LANES).astype(BF16)
    )

    pl.semaphore_wait(barrier, n_ad - 1 + n_tp - 1)

    row_copies = []
    for i, o in enumerate(ad_peers):
        row_copies.append(
            pltpu.make_async_remote_copy(
                src_ref=sb.at[o], dst_ref=rb.at[ad], send_sem=row_send.at[i], recv_sem=row_recv.at[i],
                device_id=(o, tp), device_id_type=MESH,
            )
        )
        row_copies[-1].start()
    own_rows = pltpu.make_async_copy(sb.at[ad], rb.at[ad], own_sem.at[0])
    own_rows.start()

    def slab_copy(src, to, n):
        return pltpu.make_async_remote_copy(
            src_ref=h_all.at[src], dst_ref=h_all.at[src], send_sem=slab_send.at[n], recv_sem=slab_recv.at[n],
            device_id=(ad, to), device_id_type=MESH,
        )

    slab_far = slab_copy(tp, far, 0)
    slab_far.start()
    slab_near = slab_copy(tp, near, 1)
    slab_near.start()

    q_copy.wait()
    k_copy.wait()
    v_copy.wait()

    lane_group = iota((heads, kv * ctx), 1)
    head_row = iota((heads, kv * ctx), 0)
    block_ok = jnp.zeros((heads, kv * ctx), jnp.bool_)
    for g in range(kv):
        block_ok = block_ok | (
            (lane_group >= g * ctx) & (lane_group < (g + 1) * ctx)
            & (head_row >= g * group) & (head_row < (g + 1) * group)
        )
    slot = lane_group
    for g in range(1, kv):
        slot = jnp.where(lane_group >= g * ctx, lane_group - g * ctx, slot)
    slot = jnp.where(block_ok, slot, ctx)

    unroll = 4

    def attend(step, carry):
        for u in range(unroll):
            b = step * unroll + u
            keys = k_s[b].reshape(kv * ctx, head)
            values = v_s[b].reshape(kv * ctx, head)
            s = dot_last(q_s[b], keys) * scale
            s = jnp.where(slot < fill_ref[b], s, -1e30)
            m = jnp.max(s, axis=1, keepdims=True)
            p = jnp.exp(s - m)
            l = jnp.sum(p, axis=1, keepdims=True)
            acc_s[b] = jnp.dot(p.astype(BF16), values, preferred_element_type=F32)
            m_s[b] = jnp.broadcast_to(m, (heads, head))
            l_s[b] = jnp.broadcast_to(l, (heads, head))
        return carry

    steps = rows // unroll
    lax.fori_loop(0, steps // 2, attend, 0)

    slab_far.wait()
    slab_on = slab_copy(far, near, 2)
    slab_on.start()

    dn_copy.wait()
    own_rows.wait()
    for c in row_copies:
        c.wait()
    wide = rb[:, :, 0:half].astype(F32).reshape(pack_rows, half)
    ids = rb[:, :, half : half + LANES].astype(F32).reshape(pack_rows, LANES)
    got = wide.astype(BF16)
    squares = jnp.sum(wide * wide, axis=1, keepdims=True)
    first = dot_last(got, dn_s[:, 0:half])
    second = dot_last(got, dn_s[:, half:slab])
    sub = iota((n_ad, 2 * CAP, LANES), 1).reshape(pack_rows, LANES)
    is_low = sub < CAP
    lane_adapter = jnp.floor(iota((pack_rows, LANES), 1).astype(F32) * (1.0 / rank))
    latent = jnp.zeros((pack_rows, LANES), F32)
    for t in range(groups):
        part = slice(t * LANES, (t + 1) * LANES)
        pick = jnp.where(is_low, first[:, part], second[:, part])
        latent = latent + jnp.where(ids == lane_adapter + t * per, pick, 0.0)
    mine_lane = lane_adapter == ids - per * jnp.floor(ids * (1.0 / per))
    msg = jnp.where(mine_lane, latent, squares).reshape(n_ad, 2 * CAP, LANES)
    pb[tp] = msg[:, 0:CAP] + msg[:, CAP : 2 * CAP]

    lat_copies = []
    for i, t in enumerate(tp_peers):
        lat_copies.append(
            pltpu.make_async_remote_copy(
                src_ref=pb.at[tp], dst_ref=pb.at[tp], send_sem=lat_send.at[i], recv_sem=lat_recv.at[i],
                device_id=(ad, t), device_id_type=MESH,
            )
        )
        lat_copies[-1].start()

    lax.fori_loop(steps // 2, steps, attend, 0)
    for c in up_copies:
        c.wait()

    for c in lat_copies:
        c.wait()
    total = pb[0]
    for t in range(1, n_tp):
        total = total + pb[t]
    total = jnp.concatenate([total, total], axis=1).reshape(pack_rows, LANES)
    square_sum = jnp.max(jnp.where(mine_lane, 0.0, total), axis=1, keepdims=True)
    latent = total * lax.rsqrt(square_sum / MODEL_WIDTH + epsilon)
    latent = jnp.dot(
        jnp.where(mine_lane, latent, 0.0).astype(BF16), parity, preferred_element_type=F32
    )
    wide_low = iota((n_ad, 2 * CAP, 2 * LANES), 1).reshape(pack_rows, 2 * LANES) < CAP
    latent = jnp.where(wide_low, latent[:, 0 : 2 * LANES], latent[:, 2 * LANES :])
    wide_ids = jnp.concatenate([ids, ids], axis=1)
    wide_adapter = jnp.floor(iota((pack_rows, 2 * LANES), 1).astype(F32) * (0.5 / rank))
    spread = jnp.concatenate(
        [jnp.where(wide_ids == wide_adapter + t * per, latent, 0.0).astype(BF16) for t in range(groups)], axis=1
    )
    up_rows = adapters * rank
    up_flat = jnp.concatenate([up_s[c].reshape(2 * up_rows, LANES) for c in range(tiles)], axis=1)
    delta = adapter_scale * jnp.dot(spread, up_flat, preferred_element_type=F32)
    db[...] = delta.reshape(n_ad, 2 * CAP, width)

    ret_copies = []
    for i, o in enumerate(ad_peers):
        ret_copies.append(
            pltpu.make_async_remote_copy(
                src_ref=db.at[o], dst_ref=ret.at[ad], send_sem=ret_send.at[i], recv_sem=ret_recv.at[i],
                device_id=(o, tp), device_id_type=MESH,
            )
        )
        ret_copies[-1].start()
    own_ret = pltpu.make_async_copy(db.at[ad], ret.at[ad], own_sem.at[1])
    own_ret.start()

    slab_near.wait()
    slab_on.wait()
    square_sum = jnp.zeros((rows, 1), F32)
    for t in range(n_tp):
        x = h_all[t].astype(F32)
        square_sum = square_sum + jnp.sum(x * x, axis=1, keepdims=True)
    inverse = lax.rsqrt(square_sum / MODEL_WIDTH + epsilon)
    base = jnp.zeros((2 * rows, width), F32)
    piece = slab // 4
    for t in range(n_tp):
        normed = (h_all[t].astype(F32) * inverse).astype(BF16)
        for j in range(slab // LANES):
            at = 2 * (t * slab + j * LANES)
            both = jnp.dot(normed[:, j * LANES : (j + 1) * LANES], parity, preferred_element_type=F32).astype(BF16)
            lhs_s[0:rows, at : at + 2 * LANES] = both[:, 0 : 2 * LANES]
            lhs_s[rows : 2 * rows, at : at + 2 * LANES] = both[:, 2 * LANES :]
    for t in range(n_tp):
        for c in range(tiles):
            w_copies[t * tiles + c].wait()
        for j in range(4):
            at = t * slab + j * piece
            flat = jnp.concatenate(
                [w_s[c, at : at + piece].reshape(2 * piece, LANES) for c in range(tiles)], axis=1
            )
            base = base + jnp.dot(lhs_s[:, 2 * at : 2 * (at + piece)], flat, preferred_element_type=F32)

    pick_id = iota((rows, pack_rows), 1).astype(F32)
    own_ret.wait()
    for c in ret_copies:
        c.wait()
    back = ret[...].reshape(pack_rows, width)
    pick = jnp.concatenate(
        [jnp.where(pick_id == target_c + kind * CAP, 1.0, 0.0) for kind in range(2)], axis=0
    )
    moved = jnp.dot(pick, back, precision=lax.Precision.HIGHEST, preferred_element_type=F32)
    new = (base + moved).astype(BF16)
    app_ref[0] = new[0:rows]
    app_ref[1] = new[rows : 2 * rows]
    new = new.astype(F32)
    fresh = (new[0:rows], new[rows : 2 * rows])
    for b in range(rows):
        key_rows, value_rows = (
            jnp.concatenate(
                [jnp.broadcast_to(f[b : b + 1, g * head : (g + 1) * head], (group, head)) for g in range(kv)], axis=0
            )
            for f in fresh
        )
        own = jnp.sum(q_s[b].astype(F32) * key_rows, axis=1, keepdims=True) * scale
        m = m_s[b]
        top = jnp.maximum(m, own)
        keep = jnp.exp(m - top)
        own_exp = jnp.exp(own - top)
        ctx_ref[b] = ((acc_s[b] * keep + own_exp * value_rows) / (l_s[b] * keep + own_exp)).astype(BF16)


def on_device(n_ad, n_tp, hidden, queries, keys, values, fill, choice, weight, down, up):
    rows, slab = hidden.shape
    adapters, rank, _ = down.shape
    width = up.shape[3]
    heads, head = queries.shape[1:]
    kv = keys.shape[1]
    pack_rows = 2 * CAP
    any_spec = pl.BlockSpec(memory_space=pl.ANY)
    vmem = pl.BlockSpec(memory_space=pltpu.VMEM)
    app, ctx = pl.pallas_call(
        functools.partial(kernel, n_ad, n_tp, rank),
        out_shape=(
            jax.ShapeDtypeStruct((2, rows, width), BF16),
            jax.ShapeDtypeStruct(queries.shape, BF16),
        ),
        in_specs=[vmem, pl.BlockSpec(memory_space=pltpu.SMEM)] + [any_spec] * 7,
        out_specs=(vmem, vmem),
        scratch_shapes=[
            pltpu.VMEM((n_tp, rows, slab), BF16),
            pltpu.VMEM(queries.shape, BF16),
            pltpu.VMEM(keys.shape, BF16),
            pltpu.VMEM(values.shape, BF16),
            pltpu.VMEM((width // LANES, weight.shape[0], 2, LANES), BF16),
            pltpu.VMEM((adapters * rank, slab), BF16),
            pltpu.VMEM((width // LANES, adapters * rank, 2, LANES), BF16),
            pltpu.VMEM((n_ad, pack_rows, slab // 2 + LANES), BF16),
            pltpu.VMEM((n_ad, pack_rows, slab // 2 + LANES), BF16),
            pltpu.VMEM((n_tp, n_ad, CAP, LANES), F32),
            pltpu.VMEM((n_ad, pack_rows, width), F32),
            pltpu.VMEM((n_ad, pack_rows, width), F32),
            pltpu.VMEM((2 * rows, 2 * weight.shape[0]), BF16),
            pltpu.VMEM(queries.shape, F32),
            pltpu.VMEM(queries.shape, F32),
            pltpu.VMEM(queries.shape, F32),
            pltpu.SemaphoreType.DMA((5,)),
            pltpu.SemaphoreType.DMA((n_tp * (width // LANES),)),
            pltpu.SemaphoreType.DMA((width // LANES,)),
            pltpu.SemaphoreType.DMA((2,)),
            pltpu.SemaphoreType.DMA((3,)),
            pltpu.SemaphoreType.DMA((3,)),
            pltpu.SemaphoreType.DMA((n_ad - 1,)),
            pltpu.SemaphoreType.DMA((n_ad - 1,)),
            pltpu.SemaphoreType.DMA((n_tp - 1,)),
            pltpu.SemaphoreType.DMA((n_tp - 1,)),
            pltpu.SemaphoreType.DMA((n_ad - 1,)),
            pltpu.SemaphoreType.DMA((n_ad - 1,)),
        ],
        compiler_params=pltpu.CompilerParams(
            collective_id=0, has_side_effects=True, vmem_limit_bytes=58 * 1024 * 1024
        ),
    )(
        choice.reshape(1, rows), fill, hidden, queries, keys, values,
        weight,
        down.reshape(adapters * rank, slab),
        up.reshape(adapters * rank, 2, width),
    )
    return app.reshape(2, rows, kv, head).transpose(1, 0, 2, 3), ctx


def solution(mesh):
    placed = (
        P("ad", "tp"),
        P("ad", "tp", None),
        P("ad", "tp", None, None),
        P("ad", "tp", None, None),
        P("ad"),
        P("ad"),
        P(None, None, "tp"),
        P("ad", None, "tp"),
        P("ad", None, None, "tp"),
    )
    return jax.shard_map(
        functools.partial(on_device, mesh.shape["ad"], mesh.shape["tp"]),
        mesh=mesh,
        in_specs=placed,
        out_specs=(P("ad", None, "tp", None), P("ad", "tp", None)),
        check_vma=False,
    )
```

profile of v0, /device:TPU:0, one launch (start us, length us, event | category | flops | bytes accessed | tf_op | source)
XLA Modules:
  0.0 28.6 jit_solution(16896667949794667215)
XLA Ops:
  0.6 25.0 %shard_map.104 = (bf16[2,32,256]{2,1,0:T(8,128)(2,1)}, bf16[32,16,128]{2,1,0:T(8,128)(2,1)}) custom-call(s32[1,32]{1,0:T(1,128)} %bitcast.9, s32[32]{0:T(128)} %fill_ref.1, bf16[32,2048]{1,0:T(8,128)(2,1)} %hid_in.1, bf16[32,16,128]{2,1,0:T(8,128)(2,1)} %q_in.1, bf16[32,2,128,128]{3,2,1,0:T(8,128)(2,1)} %k_in.1, bf16[32,2,128,128]{3,2,1,0:T(8,128)(2,1)} %v_in.1, ...), custom_call_target="tpu_custom_call" | custom-call | tf_op jit(solution)/shard_map/pallas_call | solution.py:330
  25.6 0.8 %reshape.19 = bf16[2,32,2,128]{3,2,1,0:T(2,128)(2,1)S(1)} reshape(bf16[2,32,256]{2,1,0:T(8,128)(2,1)} %get-tuple-element.4) | data formatting | bytes 65536 | tf_op jit(solution)/shard_map/reshape | solution.py:377
  26.4 0.6 %copy.13 = bf16[2,32,2,128]{3,2,0,1:T(2,128)(2,1)} copy(bf16[2,32,2,128]{3,2,1,0:T(2,128)(2,1)S(1)} %reshape.19) | data formatting | bytes 65536 | tf_op jit(solution)/shard_map/reshape | solution.py:377
  27.0 1.6 %copy.15 = bf16[32,16,128]{2,1,0:T(8,128)(2,1)} copy(bf16[32,16,128]{2,1,0:T(8,128)(2,1)} %get-tuple-element.9) | data formatting | bytes 262144
where the time goes:
time: 28.8 us; the launch traced here: 28.6 us
  Pallas kernels  25 us (87%)
  local copies, waits for them, and re-layouts  2.98 us (10%)
  between operations  0.64 us (2%)
    pallas_call x1, Pallas kernels, on_device(): pl.pallas_call(functools.partial(kernel, n_ad, n_tp, rank), out_shape=(ja...  25 us
    unnamed x1, local copies, waits for them, and re-layouts  1.57 us
    reshape x2, local copies, waits for them, and re-layouts, on_device(): return (app.reshape(2, rows, kv, head).transpose(1, 0, 2, 3), ctx)  1.41 us

commit v1 on v0

--- a/solution.py
+++ b/solution.py
@@ -25,12 +25,22 @@
     return lax.dot_general(a, b, (((1,), (1,)), ((), ())), preferred_element_type=F32)
 
 
+def columns(flat):
+    n = flat.shape[0] // 32
+    runs = flat.reshape(n, 2, 16, LANES)
+    first, second = runs[:, 0], runs[:, 1]
+    even = lax.rem(iota((n, 16, LANES), 1), 4) < 2
+    left = jnp.where(even, first, pltpu.roll(second, 2, 1))
+    right = jnp.where(even, pltpu.roll(first, 14, 1), second)
+    return jnp.concatenate([left.reshape(n * 16, LANES), right.reshape(n * 16, LANES)], axis=1)
+
+
 def kernel(
-    n_ad, n_tp, rank, idx_ref, fill_ref, hid_in, q_in, k_in, v_in, w_in, dn_in, up_in,
+    n_ad, n_tp, rank, width, idx_in, fill_in, hid_in, q_in, k_in, v_in, w_in, dn_in, up_in,
     app_ref, ctx_ref,
-    h_all, q_s, k_s, v_s, w_s, dn_s, up_s,
-    sb, rb, pb, db, ret, lhs_s, acc_s, m_s, l_s,
-    in_sem, w_sem, up_sem, own_sem,
+    idx_ref, fill_ref, h_all, q_s, k_s, v_s, w_s, dn_s, up_s,
+    sb, rb, pb, db, ret, lhs_s, acc_s, m_s, l_s, p_s,
+    in_sem, w_sem, own_sem,
     slab_send, slab_recv, row_send, row_recv, lat_send, lat_recv, ret_send, ret_recv,
 ):
     ad = lax.axis_index("ad")
@@ -41,8 +51,6 @@
     adapters = dn_in.shape[0] // rank
     per = LANES // rank
     groups = adapters // per
-    width = w_in.shape[2]
-    tiles = width // LANES
     head = q_in.shape[2]
     heads = q_in.shape[1]
     kv = k_in.shape[1]
@@ -50,27 +58,6 @@
     ctx = k_in.shape[2]
     scale = head ** (-0.5)
 
-    hid_copy = pltpu.make_async_copy(hid_in, h_all.at[tp], in_sem.at[0])
-    q_copy = pltpu.make_async_copy(q_in, q_s, in_sem.at[1])
-    k_copy = pltpu.make_async_copy(k_in, k_s, in_sem.at[2])
-    v_copy = pltpu.make_async_copy(v_in, v_s, in_sem.at[3])
-    dn_copy = pltpu.make_async_copy(dn_in, dn_s, in_sem.at[4])
-    up_copies = [
-        pltpu.make_async_copy(up_in.at[:, :, pl.ds(c * LANES, LANES)], up_s.at[c], up_sem.at[c])
-        for c in range(tiles)
-    ]
-    w_copies = [
-        pltpu.make_async_copy(
-            w_in.at[pl.ds(i * slab, slab), :, pl.ds(c * LANES, LANES)],
-            w_s.at[c, pl.ds(i * slab, slab)],
-            w_sem.at[i * tiles + c],
-        )
-        for i in range(n_tp)
-        for c in range(tiles)
-    ]
-    for c in (hid_copy, q_copy, k_copy, v_copy, dn_copy, *up_copies, *w_copies):
-        c.start()
-
     ad_peers = [lax.rem(ad + i, n_ad) for i in range(1, n_ad)]
     tp_peers = [lax.rem(tp + i, n_tp) for i in range(1, n_tp)]
     far = lax.rem(tp + 2, n_tp)
@@ -82,16 +69,36 @@
     for t in tp_peers:
         pl.semaphore_signal(barrier, inc=1, device_id=(ad, t), device_id_type=MESH)
 
+    idx_copy = pltpu.make_async_copy(idx_in, idx_ref, in_sem.at[5])
+    hid_copy = pltpu.make_async_copy(hid_in, h_all.at[tp], in_sem.at[0])
+    fill_copy = pltpu.make_async_copy(fill_in, fill_ref, in_sem.at[6])
+    q_copy = pltpu.make_async_copy(q_in, q_s, in_sem.at[1])
+    k_copy = pltpu.make_async_copy(k_in, k_s, in_sem.at[2])
+    v_copy = pltpu.make_async_copy(v_in, v_s, in_sem.at[3])
+    dn_copy = pltpu.make_async_copy(dn_in, dn_s, in_sem.at[4])
+    up_copy = pltpu.make_async_copy(up_in, up_s, in_sem.at[7])
+    flat_slab = w_in.shape[0] // n_tp
+    w_copies = [
+        pltpu.make_async_copy(
+            w_in.at[pl.ds(i * flat_slab, flat_slab)], w_s.at[pl.ds(i * flat_slab, flat_slab)], w_sem.at[i]
+        )
+        for i in range(n_tp)
+    ]
+    for c in (idx_copy, hid_copy, fill_copy, q_copy, k_copy, v_copy, dn_copy, up_copy):
+        c.start()
+
+    lane = iota((LANES, 2 * LANES), 0)
+    eighth = lax.rem(lane, 8)
+    place = 2 * (lane - eighth) + jnp.where(eighth < 4, 4 * eighth, 4 * eighth - 14)
     parity = jnp.concatenate(
         [
-            jnp.where(
-                iota((LANES, 2 * LANES), 1) == 2 * iota((LANES, 2 * LANES), 0) + kind, 1.0, 0.0
-            ).astype(BF16)
+            jnp.where(iota((LANES, 2 * LANES), 1) == place + kind, 1.0, 0.0).astype(BF16)
             for kind in range(2)
         ],
         axis=1,
     )
 
+    idx_copy.wait()
     idx_r = jnp.broadcast_to(idx_ref[...].astype(F32), (rows, rows))
     eye = iota((rows, rows), 0) == iota((rows, rows), 1)
     idx_c = jnp.sum(jnp.where(eye, idx_r, 0.0), axis=1, keepdims=True)
@@ -151,9 +158,12 @@
     slab_near = slab_copy(tp, near, 1)
     slab_near.start()
 
+    fill_copy.wait()
     q_copy.wait()
     k_copy.wait()
     v_copy.wait()
+    for c in w_copies:
+        c.start()
 
     lane_group = iota((heads, kv * ctx), 1)
     head_row = iota((heads, kv * ctx), 0)
@@ -168,25 +178,19 @@
         slot = jnp.where(lane_group >= g * ctx, lane_group - g * ctx, slot)
     slot = jnp.where(block_ok, slot, ctx)
 
-    unroll = 4
-
-    def attend(step, carry):
-        for u in range(unroll):
-            b = step * unroll + u
-            keys = k_s[b].reshape(kv * ctx, head)
-            values = v_s[b].reshape(kv * ctx, head)
-            s = dot_last(q_s[b], keys) * scale
-            s = jnp.where(slot < fill_ref[b], s, -1e30)
-            m = jnp.max(s, axis=1, keepdims=True)
-            p = jnp.exp(s - m)
-            l = jnp.sum(p, axis=1, keepdims=True)
-            acc_s[b] = jnp.dot(p.astype(BF16), values, preferred_element_type=F32)
-            m_s[b] = jnp.broadcast_to(m, (heads, head))
-            l_s[b] = jnp.broadcast_to(l, (heads, head))
-        return carry
-
-    steps = rows // unroll
-    lax.fori_loop(0, steps // 2, attend, 0)
+    for b in range(rows):
+        p_s[b] = jnp.where(
+            slot < fill_ref[b], dot_last(q_s[b], k_s[b].reshape(kv * ctx, head)) * scale, -1e30
+        )
+    for b in range(rows):
+        s = p_s[b]
+        m = jnp.max(s, axis=1, keepdims=True)
+        p = jnp.exp(s - m)
+        p_s[b] = p
+        m_s[b] = jnp.broadcast_to(m, (heads, head))
+        l_s[b] = jnp.broadcast_to(jnp.sum(p, axis=1, keepdims=True), (heads, head))
+    for b in range(rows):
+        acc_s[b] = jnp.dot(p_s[b].astype(BF16), v_s[b].reshape(kv * ctx, head), preferred_element_type=F32)
 
     slab_far.wait()
     slab_on = slab_copy(far, near, 2)
@@ -224,9 +228,24 @@
         )
         lat_copies[-1].start()
 
-    lax.fori_loop(steps // 2, steps, attend, 0)
-    for c in up_copies:
-        c.wait()
+    slab_near.wait()
+    slab_on.wait()
+    square_sum = jnp.zeros((rows, 1), F32)
+    for t in range(n_tp):
+        x = h_all[t].astype(F32)
+        square_sum = square_sum + jnp.sum(x * x, axis=1, keepdims=True)
+    inverse = lax.rsqrt(square_sum / MODEL_WIDTH + epsilon)
+    for t in range(n_tp):
+        normed = (h_all[t].astype(F32) * inverse).astype(BF16)
+        stack = jnp.concatenate([normed[:, j * LANES : (j + 1) * LANES] for j in range(slab // LANES)], axis=0)
+        wide_rows = jnp.dot(stack, parity, preferred_element_type=F32).astype(BF16)
+        for j in range(slab // LANES):
+            at = 2 * (t * slab + j * LANES)
+            both = wide_rows[j * rows : (j + 1) * rows]
+            lhs_s[0:rows, at : at + 2 * LANES] = both[:, 0 : 2 * LANES]
+            lhs_s[rows : 2 * rows, at : at + 2 * LANES] = both[:, 2 * LANES :]
+    up_copy.wait()
+    up_flat = columns(up_s[...])
 
     for c in lat_copies:
         c.wait()
@@ -246,8 +265,6 @@
     spread = jnp.concatenate(
         [jnp.where(wide_ids == wide_adapter + t * per, latent, 0.0).astype(BF16) for t in range(groups)], axis=1
     )
-    up_rows = adapters * rank
-    up_flat = jnp.concatenate([up_s[c].reshape(2 * up_rows, LANES) for c in range(tiles)], axis=1)
     delta = adapter_scale * jnp.dot(spread, up_flat, preferred_element_type=F32)
     db[...] = delta.reshape(n_ad, 2 * CAP, width)
 
@@ -263,30 +280,13 @@
     own_ret = pltpu.make_async_copy(db.at[ad], ret.at[ad], own_sem.at[1])
     own_ret.start()
 
-    slab_near.wait()
-    slab_on.wait()
-    square_sum = jnp.zeros((rows, 1), F32)
-    for t in range(n_tp):
-        x = h_all[t].astype(F32)
-        square_sum = square_sum + jnp.sum(x * x, axis=1, keepdims=True)
-    inverse = lax.rsqrt(square_sum / MODEL_WIDTH + epsilon)
     base = jnp.zeros((2 * rows, width), F32)
     piece = slab // 4
     for t in range(n_tp):
-        normed = (h_all[t].astype(F32) * inverse).astype(BF16)
-        for j in range(slab // LANES):
-            at = 2 * (t * slab + j * LANES)
-            both = jnp.dot(normed[:, j * LANES : (j + 1) * LANES], parity, preferred_element_type=F32).astype(BF16)
-            lhs_s[0:rows, at : at + 2 * LANES] = both[:, 0 : 2 * LANES]
-            lhs_s[rows : 2 * rows, at : at + 2 * LANES] = both[:, 2 * LANES :]
-    for t in range(n_tp):
-        for c in range(tiles):
-            w_copies[t * tiles + c].wait()
+        w_copies[t].wait()
         for j in range(4):
             at = t * slab + j * piece
-            flat = jnp.concatenate(
-                [w_s[c, at : at + piece].reshape(2 * piece, LANES) for c in range(tiles)], axis=1
-            )
+            flat = columns(w_s[4 * at : 4 * (at + piece)])
             base = base + jnp.dot(lhs_s[:, 2 * at : 2 * (at + piece)], flat, preferred_element_type=F32)
 
     pick_id = iota((rows, pack_rows), 1).astype(F32)
@@ -318,6 +318,11 @@
         ctx_ref[b] = ((acc_s[b] * keep + own_exp * value_rows) / (l_s[b] * keep + own_exp)).astype(BF16)
 
 
+def by_tile(a):
+    tiles = a.shape[-1] // LANES
+    return a.reshape(-1, 2, tiles, LANES).transpose(0, 2, 1, 3).reshape(-1, LANES)
+
+
 def on_device(n_ad, n_tp, hidden, queries, keys, values, fill, choice, weight, down, up):
     rows, slab = hidden.shape
     adapters, rank, _ = down.shape
@@ -328,21 +333,23 @@
     any_spec = pl.BlockSpec(memory_space=pl.ANY)
     vmem = pl.BlockSpec(memory_space=pltpu.VMEM)
     app, ctx = pl.pallas_call(
-        functools.partial(kernel, n_ad, n_tp, rank),
+        functools.partial(kernel, n_ad, n_tp, rank, width),
         out_shape=(
             jax.ShapeDtypeStruct((2, rows, width), BF16),
             jax.ShapeDtypeStruct(queries.shape, BF16),
         ),
-        in_specs=[vmem, pl.BlockSpec(memory_space=pltpu.SMEM)] + [any_spec] * 7,
+        in_specs=[any_spec] * 9,
         out_specs=(vmem, vmem),
         scratch_shapes=[
+            pltpu.VMEM((1, rows), jnp.int32),
+            pltpu.SMEM((rows,), jnp.int32),
             pltpu.VMEM((n_tp, rows, slab), BF16),
             pltpu.VMEM(queries.shape, BF16),
             pltpu.VMEM(keys.shape, BF16),
             pltpu.VMEM(values.shape, BF16),
-            pltpu.VMEM((width // LANES, weight.shape[0], 2, LANES), BF16),
+            pltpu.VMEM((4 * weight.shape[0], LANES), BF16),
             pltpu.VMEM((adapters * rank, slab), BF16),
-            pltpu.VMEM((width // LANES, adapters * rank, 2, LANES), BF16),
+            pltpu.VMEM((4 * adapters * rank, LANES), BF16),
             pltpu.VMEM((n_ad, pack_rows, slab // 2 + LANES), BF16),
             pltpu.VMEM((n_ad, pack_rows, slab // 2 + LANES), BF16),
             pltpu.VMEM((n_tp, n_ad, CAP, LANES), F32),
@@ -352,9 +359,9 @@
             pltpu.VMEM(queries.shape, F32),
             pltpu.VMEM(queries.shape, F32),
             pltpu.VMEM(queries.shape, F32),
-            pltpu.SemaphoreType.DMA((5,)),
-            pltpu.SemaphoreType.DMA((n_tp * (width // LANES),)),
-            pltpu.SemaphoreType.DMA((width // LANES,)),
+            pltpu.VMEM((rows, heads, kv * keys.shape[2]), F32),
+            pltpu.SemaphoreType.DMA((8,)),
+            pltpu.SemaphoreType.DMA((n_tp,)),
             pltpu.SemaphoreType.DMA((2,)),
             pltpu.SemaphoreType.DMA((3,)),
             pltpu.SemaphoreType.DMA((3,)),
@@ -366,15 +373,34 @@
             pltpu.SemaphoreType.DMA((n_ad - 1,)),
         ],
         compiler_params=pltpu.CompilerParams(
-            collective_id=0, has_side_effects=True, vmem_limit_bytes=58 * 1024 * 1024
+            collective_id=0, has_side_effects=True, vmem_limit_bytes=40 * 1024 * 1024
         ),
-    )(
-        choice.reshape(1, rows), fill, hidden, queries, keys, values,
-        weight,
-        down.reshape(adapters * rank, slab),
-        up.reshape(adapters * rank, 2, width),
-    )
-    return app.reshape(2, rows, kv, head).transpose(1, 0, 2, 3), ctx
+    )(*[
+        pltpu.with_memory_space_constraint(x, pltpu.HBM)
+        for x in (
+            choice.reshape(1, rows), fill, hidden, queries, keys, values,
+            by_tile(weight),
+            down.reshape(adapters * rank, slab),
+            by_tile(up),
+        )
+    ])
+
+    def finish(app_ref, ctx_ref, app_out, ctx_out):
+        for kind in range(2):
+            for g in range(kv):
+                app_out[:, kind, g, :] = app_ref[kind, :, g * head : (g + 1) * head]
+        ctx_out[...] = ctx_ref[...]
+
+    return pl.pallas_call(
+        finish,
+        out_shape=(
+            jax.ShapeDtypeStruct((rows, 2, kv, head), BF16),
+            jax.ShapeDtypeStruct(queries.shape, BF16),
+        ),
+        in_specs=[vmem] * 2,
+        out_specs=(vmem, vmem),
+        compiler_params=pltpu.CompilerParams(vmem_limit_bytes=4 * 1024 * 1024),
+    )(app, ctx)
 
 
 def solution(mesh):

time: 28.8 us -> 23.4 us (0.81)
  local copies, waits for them, and re-layouts: 2.98 us -> 0 us
  Pallas kernels: 25 us -> 22.6 us
    pallas_call x1 -> x2, Pallas kernels: 25 us -> 22.6 us  [the longest x1 21.9 us: on_device(): pl.pallas_call(functools.partial(kernel, n_ad, n_tp, rank, width), out_sh...]
    unnamed x1 -> x0, local copies, waits for them, and re-layouts: 1.57 us -> none
    reshape x2 -> x0, local copies, waits for them, and re-layouts: 1.41 us -> none  [on_device(): return (app.reshape(2, rows, kv, head).transpose(1, 0, 2, 3), ctx)]
where the time goes in v1:
time: 23.4 us; the launch traced here: 23.2 us
  Pallas kernels  22.6 us (97%)
  between operations  0.64 us (3%)
    pallas_call x1, Pallas kernels, on_device(): pl.pallas_call(functools.partial(kernel, n_ad, n_tp, rank, width), out_sh...  21.9 us
    pallas_call x1, Pallas kernels, on_device(): pl.pallas_call(finish, out_shape=(jax.ShapeDtypeStruct((rows, 2, kv, head...  0.7 us

profile of v1, /device:TPU:0, one launch (start us, length us, event | category | flops | bytes accessed | tf_op | source)
XLA Modules:
  0.0 23.2 jit_solution(4211272497284788622)
XLA Ops:
  0.6 21.9 %shard_map.104 = (bf16[2,32,256]{2,1,0:T(8,128)(2,1)S(1)}, bf16[32,16,128]{2,1,0:T(8,128)(2,1)S(1)}) custom-call(s32[1,32]{1,0:T(1,128)} %bitcast.15, s32[32]{0:T(128)} %fill_in.1, bf16[32,2048]{1,0:T(8,128)(2,1)} %hid_in.1, bf16[32,16,128]{2,1,0:T(8,128)(2,1)} %q_in.1, bf16[32,2,128,128]{3,2,1,0:T(8,128)(2,1)} %k_in.1, bf16[32,2,128,128]{3,2,1,0:T(8,128)(2,1)} %v_in.1, ...), custom_call_target="tpu_custom_call" | custom-call | tf_op jit(solution)/shard_map/pallas_call | solution.py:335
  22.5 0.7 %shard_map.105 = (bf16[32,2,2,128]{3,2,1,0:T(2,128)(2,1)}, bf16[32,16,128]{2,1,0:T(8,128)(2,1)}) custom-call(bf16[2,32,256]{2,1,0:T(8,128)(2,1)S(1)} %get-tuple-element.4.app_ref, bf16[32,16,128]{2,1,0:T(8,128)(2,1)S(1)} %get-tuple-element.5.ctx_ref), custom_call_target="tpu_custom_call" | custom-call | tf_op jit(solution)/shard_map/pallas_call | solution.py:394

commit v2 on v1

--- a/solution.py
+++ b/solution.py
@@ -35,13 +35,16 @@
     return jnp.concatenate([left.reshape(n * 16, LANES), right.reshape(n * 16, LANES)], axis=1)
 
 
+def landed(ref, sem):
+    pltpu.make_async_copy(ref, ref, sem).wait()
+
+
 def kernel(
     n_ad, n_tp, rank, width, idx_in, fill_in, hid_in, q_in, k_in, v_in, w_in, dn_in, up_in,
     app_ref, ctx_ref,
-    idx_ref, fill_ref, h_all, q_s, k_s, v_s, w_s, dn_s, up_s,
+    idx_ref, fill_ref, h_all, q_s, k_s, v_s, w_s, dn_s, dn_t, up_s,
     sb, rb, pb, db, ret, lhs_s, acc_s, m_s, l_s, p_s,
-    in_sem, w_sem, own_sem,
-    slab_send, slab_recv, row_send, row_recv, lat_send, lat_recv, ret_send, ret_recv,
+    in_sem, w_sem, slab_sem, row_sem, lat_sem, ret_sem,
 ):
     ad = lax.axis_index("ad")
     tp = lax.axis_index("tp")
@@ -58,7 +61,7 @@
     ctx = k_in.shape[2]
     scale = head ** (-0.5)
 
-    ad_peers = [lax.rem(ad + i, n_ad) for i in range(1, n_ad)]
+    ad_peers = [lax.rem(ad + i, n_ad) for i in range(n_ad - 1, 0, -1)]
     tp_peers = [lax.rem(tp + i, n_tp) for i in range(1, n_tp)]
     far = lax.rem(tp + 2, n_tp)
     near = tp + 1 - 2 * lax.rem(tp, 2)
@@ -128,7 +131,8 @@
     packed = jnp.dot(low.astype(BF16), mine[:, :half], preferred_element_type=F32) + jnp.dot(
         high.astype(BF16), mine[:, half:], preferred_element_type=F32
     )
-    sb[:, :, 0:half] = packed.reshape(n_ad, 2 * CAP, half).astype(BF16)
+    packed = packed.reshape(n_ad, 2 * CAP, half).astype(BF16)
+    sb[:, :, 0:half] = packed
     sb[:, :, half : half + LANES] = (
         jnp.broadcast_to(ids_out, (pack_rows, LANES)).reshape(n_ad, 2 * CAP, LANES).astype(BF16)
     )
@@ -139,17 +143,17 @@
     for i, o in enumerate(ad_peers):
         row_copies.append(
             pltpu.make_async_remote_copy(
-                src_ref=sb.at[o], dst_ref=rb.at[ad], send_sem=row_send.at[i], recv_sem=row_recv.at[i],
+                src_ref=sb.at[o], dst_ref=rb.at[ad], send_sem=row_sem.at[0], recv_sem=row_sem.at[1],
                 device_id=(o, tp), device_id_type=MESH,
             )
         )
         row_copies[-1].start()
-    own_rows = pltpu.make_async_copy(sb.at[ad], rb.at[ad], own_sem.at[0])
+    own_rows = pltpu.make_async_copy(sb.at[ad], rb.at[ad], row_sem.at[1])
     own_rows.start()
 
     def slab_copy(src, to, n):
         return pltpu.make_async_remote_copy(
-            src_ref=h_all.at[src], dst_ref=h_all.at[src], send_sem=slab_send.at[n], recv_sem=slab_recv.at[n],
+            src_ref=h_all.at[src], dst_ref=h_all.at[src], send_sem=slab_sem.at[3], recv_sem=slab_sem.at[n],
             device_id=(ad, to), device_id_type=MESH,
         )
 
@@ -192,23 +196,24 @@
     for b in range(rows):
         acc_s[b] = jnp.dot(p_s[b].astype(BF16), v_s[b].reshape(kv * ctx, head), preferred_element_type=F32)
 
-    slab_far.wait()
+    dn_copy.wait()
+    for j in range(slab // LANES):
+        dn_t[j * LANES : (j + 1) * LANES] = dn_s[:, j * LANES : (j + 1) * LANES].T
+
+    slab_far.wait_recv()
     slab_on = slab_copy(far, near, 2)
     slab_on.start()
 
-    dn_copy.wait()
-    own_rows.wait()
-    for c in row_copies:
-        c.wait()
+    sub = iota((n_ad, 2 * CAP, LANES), 1).reshape(pack_rows, LANES)
+    is_low = sub < CAP
+    lane_adapter = jnp.floor(iota((pack_rows, LANES), 1).astype(F32) * (1.0 / rank))
+    landed(rb, row_sem.at[1])
     wide = rb[:, :, 0:half].astype(F32).reshape(pack_rows, half)
     ids = rb[:, :, half : half + LANES].astype(F32).reshape(pack_rows, LANES)
     got = wide.astype(BF16)
+    first = jnp.dot(got, dn_t[0:half], preferred_element_type=F32)
+    second = jnp.dot(got, dn_t[half:slab], preferred_element_type=F32)
     squares = jnp.sum(wide * wide, axis=1, keepdims=True)
-    first = dot_last(got, dn_s[:, 0:half])
-    second = dot_last(got, dn_s[:, half:slab])
-    sub = iota((n_ad, 2 * CAP, LANES), 1).reshape(pack_rows, LANES)
-    is_low = sub < CAP
-    lane_adapter = jnp.floor(iota((pack_rows, LANES), 1).astype(F32) * (1.0 / rank))
     latent = jnp.zeros((pack_rows, LANES), F32)
     for t in range(groups):
         part = slice(t * LANES, (t + 1) * LANES)
@@ -222,14 +227,14 @@
     for i, t in enumerate(tp_peers):
         lat_copies.append(
             pltpu.make_async_remote_copy(
-                src_ref=pb.at[tp], dst_ref=pb.at[tp], send_sem=lat_send.at[i], recv_sem=lat_recv.at[i],
+                src_ref=pb.at[tp], dst_ref=pb.at[tp], send_sem=lat_sem.at[0], recv_sem=lat_sem.at[1],
                 device_id=(ad, t), device_id_type=MESH,
             )
         )
         lat_copies[-1].start()
 
-    slab_near.wait()
-    slab_on.wait()
+    slab_near.wait_recv()
+    slab_on.wait_recv()
     square_sum = jnp.zeros((rows, 1), F32)
     for t in range(n_tp):
         x = h_all[t].astype(F32)
@@ -245,39 +250,44 @@
             lhs_s[0:rows, at : at + 2 * LANES] = both[:, 0 : 2 * LANES]
             lhs_s[rows : 2 * rows, at : at + 2 * LANES] = both[:, 2 * LANES :]
     up_copy.wait()
-    up_flat = columns(up_s[...])
-
-    for c in lat_copies:
-        c.wait()
+    up_both = [[], []]
+    for t in range(groups):
+        flat = columns(up_s[4 * t * LANES : 4 * (t + 1) * LANES])
+        for kind in range(2):
+            up_both[kind].append(
+                lax.dot_general(
+                    parity[:, 2 * kind * LANES : 2 * (kind + 1) * LANES], flat, (((1,), (0,)), ((), ())),
+                    preferred_element_type=F32,
+                ).astype(BF16)
+            )
+    up_both = [jnp.concatenate(u, axis=0) for u in up_both]
+
+    landed(pb.at[pl.ds(0, n_tp - 1)], lat_sem.at[1])
     total = pb[0]
     for t in range(1, n_tp):
         total = total + pb[t]
     total = jnp.concatenate([total, total], axis=1).reshape(pack_rows, LANES)
     square_sum = jnp.max(jnp.where(mine_lane, 0.0, total), axis=1, keepdims=True)
     latent = total * lax.rsqrt(square_sum / MODEL_WIDTH + epsilon)
-    latent = jnp.dot(
-        jnp.where(mine_lane, latent, 0.0).astype(BF16), parity, preferred_element_type=F32
-    )
-    wide_low = iota((n_ad, 2 * CAP, 2 * LANES), 1).reshape(pack_rows, 2 * LANES) < CAP
-    latent = jnp.where(wide_low, latent[:, 0 : 2 * LANES], latent[:, 2 * LANES :])
-    wide_ids = jnp.concatenate([ids, ids], axis=1)
-    wide_adapter = jnp.floor(iota((pack_rows, 2 * LANES), 1).astype(F32) * (0.5 / rank))
+    latent = jnp.where(mine_lane, latent, 0.0).astype(BF16)
     spread = jnp.concatenate(
-        [jnp.where(wide_ids == wide_adapter + t * per, latent, 0.0).astype(BF16) for t in range(groups)], axis=1
-    )
-    delta = adapter_scale * jnp.dot(spread, up_flat, preferred_element_type=F32)
-    db[...] = delta.reshape(n_ad, 2 * CAP, width)
+        [jnp.where(ids == lane_adapter + t * per, latent, jnp.zeros_like(latent)) for t in range(groups)], axis=1
+    )
+    key_delta, value_delta = (jnp.dot(spread, u, preferred_element_type=F32) for u in up_both)
+    is_key = iota((n_ad, 2 * CAP, width), 1).reshape(pack_rows, width) < CAP
+    delta = adapter_scale * jnp.where(is_key, key_delta, value_delta)
+    db[...] = delta.reshape(n_ad, 2 * CAP, width).astype(BF16)
 
     ret_copies = []
     for i, o in enumerate(ad_peers):
         ret_copies.append(
             pltpu.make_async_remote_copy(
-                src_ref=db.at[o], dst_ref=ret.at[ad], send_sem=ret_send.at[i], recv_sem=ret_recv.at[i],
+                src_ref=db.at[o], dst_ref=ret.at[ad], send_sem=ret_sem.at[0], recv_sem=ret_sem.at[1],
                 device_id=(o, tp), device_id_type=MESH,
             )
         )
         ret_copies[-1].start()
-    own_ret = pltpu.make_async_copy(db.at[ad], ret.at[ad], own_sem.at[1])
+    own_ret = pltpu.make_async_copy(db.at[ad], ret.at[ad], ret_sem.at[1])
     own_ret.start()
 
     base = jnp.zeros((2 * rows, width), F32)
@@ -290,14 +300,16 @@
             base = base + jnp.dot(lhs_s[:, 2 * at : 2 * (at + piece)], flat, preferred_element_type=F32)
 
     pick_id = iota((rows, pack_rows), 1).astype(F32)
-    own_ret.wait()
-    for c in ret_copies:
-        c.wait()
-    back = ret[...].reshape(pack_rows, width)
+    landed(sb.at[pl.ds(0, n_ad - 1)], row_sem.at[0])
+    landed(pb.at[pl.ds(0, n_tp - 1)], lat_sem.at[0])
+    landed(h_all.at[pl.ds(0, n_tp - 1)], slab_sem.at[3])
+    landed(db.at[pl.ds(0, n_ad - 1)], ret_sem.at[0])
+    landed(ret, ret_sem.at[1])
+    back = ret[...].astype(F32).reshape(pack_rows, width).astype(BF16)
     pick = jnp.concatenate(
         [jnp.where(pick_id == target_c + kind * CAP, 1.0, 0.0) for kind in range(2)], axis=0
-    )
-    moved = jnp.dot(pick, back, precision=lax.Precision.HIGHEST, preferred_element_type=F32)
+    ).astype(BF16)
+    moved = jnp.dot(pick, back, preferred_element_type=F32)
     new = (base + moved).astype(BF16)
     app_ref[0] = new[0:rows]
     app_ref[1] = new[rows : 2 * rows]
@@ -349,12 +361,13 @@
             pltpu.VMEM(values.shape, BF16),
             pltpu.VMEM((4 * weight.shape[0], LANES), BF16),
             pltpu.VMEM((adapters * rank, slab), BF16),
+            pltpu.VMEM((slab, adapters * rank), BF16),
             pltpu.VMEM((4 * adapters * rank, LANES), BF16),
             pltpu.VMEM((n_ad, pack_rows, slab // 2 + LANES), BF16),
             pltpu.VMEM((n_ad, pack_rows, slab // 2 + LANES), BF16),
             pltpu.VMEM((n_tp, n_ad, CAP, LANES), F32),
-            pltpu.VMEM((n_ad, pack_rows, width), F32),
-            pltpu.VMEM((n_ad, pack_rows, width), F32),
+            pltpu.VMEM((n_ad, pack_rows, width), BF16),
+            pltpu.VMEM((n_ad, pack_rows, width), BF16),
             pltpu.VMEM((2 * rows, 2 * weight.shape[0]), BF16),
             pltpu.VMEM(queries.shape, F32),
             pltpu.VMEM(queries.shape, F32),
@@ -362,15 +375,10 @@
             pltpu.VMEM((rows, heads, kv * keys.shape[2]), F32),
             pltpu.SemaphoreType.DMA((8,)),
             pltpu.SemaphoreType.DMA((n_tp,)),
+            pltpu.SemaphoreType.DMA((4,)),
             pltpu.SemaphoreType.DMA((2,)),
-            pltpu.SemaphoreType.DMA((3,)),
-            pltpu.SemaphoreType.DMA((3,)),
-            pltpu.SemaphoreType.DMA((n_ad - 1,)),
-            pltpu.SemaphoreType.DMA((n_ad - 1,)),
-            pltpu.SemaphoreType.DMA((n_tp - 1,)),
-            pltpu.SemaphoreType.DMA((n_tp - 1,)),
-            pltpu.SemaphoreType.DMA((n_ad - 1,)),
-            pltpu.SemaphoreType.DMA((n_ad - 1,)),
+            pltpu.SemaphoreType.DMA((2,)),
+            pltpu.SemaphoreType.DMA((2,)),
         ],
         compiler_params=pltpu.CompilerParams(
             collective_id=0, has_side_effects=True, vmem_limit_bytes=40 * 1024 * 1024

time: 23.4 us -> 20.9 us (0.89)
  Pallas kernels: 22.6 us -> 20.1 us
    pallas_call x1, Pallas kernels: 21.9 us -> 19.4 us  [on_device(): pl.pallas_call(functools.partial(kernel, n_ad, n_tp, rank, width), out_sh...]
where the time goes in v2:
time: 20.9 us; the launch traced here: 20.7 us
  Pallas kernels  20.1 us (96%)
  between operations  0.64 us (3%)
    pallas_call x1, Pallas kernels, on_device(): pl.pallas_call(functools.partial(kernel, n_ad, n_tp, rank, width), out_sh...  19.4 us
    pallas_call x1, Pallas kernels, on_device(): pl.pallas_call(finish, out_shape=(jax.ShapeDtypeStruct((rows, 2, kv, head...  0.7 us

profile of v2, /device:TPU:0, one launch (start us, length us, event | category | flops | bytes accessed | tf_op | source)
XLA Modules:
  0.0 20.7 jit_solution(18017682881213404139)
XLA Ops:
  0.6 19.4 %shard_map.104 = (bf16[2,32,256]{2,1,0:T(8,128)(2,1)S(1)}, bf16[32,16,128]{2,1,0:T(8,128)(2,1)S(1)}) custom-call(s32[1,32]{1,0:T(1,128)} %bitcast.15, s32[32]{0:T(128)} %fill_in.1, bf16[32,2048]{1,0:T(8,128)(2,1)} %hid_in.1, bf16[32,16,128]{2,1,0:T(8,128)(2,1)} %q_in.1, bf16[32,2,128,128]{3,2,1,0:T(8,128)(2,1)} %k_in.1, bf16[32,2,128,128]{3,2,1,0:T(8,128)(2,1)} %v_in.1, ...), custom_call_target="tpu_custom_call" | custom-call | tf_op jit(solution)/shard_map/pallas_call | solution.py:347
  20.0 0.7 %shard_map.105 = (bf16[32,2,2,128]{3,2,1,0:T(2,128)(2,1)}, bf16[32,16,128]{2,1,0:T(8,128)(2,1)}) custom-call(bf16[2,32,256]{2,1,0:T(8,128)(2,1)S(1)} %get-tuple-element.4.app_ref, bf16[32,16,128]{2,1,0:T(8,128)(2,1)S(1)} %get-tuple-element.5.ctx_ref), custom_call_target="tpu_custom_call" | custom-call | tf_op jit(solution)/shard_map/pallas_call | solution.py:402

commit v3 on v2

--- a/solution.py
+++ b/solution.py
@@ -211,14 +211,16 @@
     wide = rb[:, :, 0:half].astype(F32).reshape(pack_rows, half)
     ids = rb[:, :, half : half + LANES].astype(F32).reshape(pack_rows, LANES)
     got = wide.astype(BF16)
-    first = jnp.dot(got, dn_t[0:half], preferred_element_type=F32)
-    second = jnp.dot(got, dn_t[half:slab], preferred_element_type=F32)
     squares = jnp.sum(wide * wide, axis=1, keepdims=True)
     latent = jnp.zeros((pack_rows, LANES), F32)
-    for t in range(groups):
-        part = slice(t * LANES, (t + 1) * LANES)
-        pick = jnp.where(is_low, first[:, part], second[:, part])
-        latent = latent + jnp.where(ids == lane_adapter + t * per, pick, 0.0)
+    for t in range(0, groups, 2):
+        cols = slice(t * LANES, (t + 2) * LANES)
+        first = jnp.dot(got, dn_t[0:half, cols], preferred_element_type=F32)
+        second = jnp.dot(got, dn_t[half:slab, cols], preferred_element_type=F32)
+        for u in range(2):
+            part = slice(u * LANES, (u + 1) * LANES)
+            pick = jnp.where(is_low, first[:, part], second[:, part])
+            latent = latent + jnp.where(ids == lane_adapter + (t + u) * per, pick, 0.0)
     mine_lane = lane_adapter == ids - per * jnp.floor(ids * (1.0 / per))
     msg = jnp.where(mine_lane, latent, squares).reshape(n_ad, 2 * CAP, LANES)
     pb[tp] = msg[:, 0:CAP] + msg[:, CAP : 2 * CAP]

time: 20.9 us -> 20.9 us (level)
  no operation moved by 1% of the time
where the time goes in v3:
time: 20.9 us; the launch traced here: 20.7 us
  Pallas kernels  20.1 us (96%)
  between operations  0.64 us (3%)
    pallas_call x1, Pallas kernels, on_device(): pl.pallas_call(functools.partial(kernel, n_ad, n_tp, rank, width), out_sh...  19.4 us
    pallas_call x1, Pallas kernels, on_device(): pl.pallas_call(finish, out_shape=(jax.ShapeDtypeStruct((rows, 2, kv, head...  0.7 us

profile of v3, /device:TPU:0, one launch (start us, length us, event | category | flops | bytes accessed | tf_op | source)
XLA Modules:
  0.0 20.7 jit_solution(7538983529380437403)
XLA Ops:
  0.6 19.4 %shard_map.104 = (bf16[2,32,256]{2,1,0:T(8,128)(2,1)S(1)}, bf16[32,16,128]{2,1,0:T(8,128)(2,1)S(1)}) custom-call(s32[1,32]{1,0:T(1,128)} %bitcast.15, s32[32]{0:T(128)} %fill_in.1, bf16[32,2048]{1,0:T(8,128)(2,1)} %hid_in.1, bf16[32,16,128]{2,1,0:T(8,128)(2,1)} %q_in.1, bf16[32,2,128,128]{3,2,1,0:T(8,128)(2,1)} %k_in.1, bf16[32,2,128,128]{3,2,1,0:T(8,128)(2,1)} %v_in.1, ...), custom_call_target="tpu_custom_call" | custom-call | tf_op jit(solution)/shard_map/pallas_call | solution.py:349
  20.0 0.7 %shard_map.105 = (bf16[32,2,2,128]{3,2,1,0:T(2,128)(2,1)}, bf16[32,16,128]{2,1,0:T(8,128)(2,1)}) custom-call(bf16[2,32,256]{2,1,0:T(8,128)(2,1)S(1)} %get-tuple-element.4.app_ref, bf16[32,16,128]{2,1,0:T(8,128)(2,1)S(1)} %get-tuple-element.5.ctx_ref), custom_call_target="tpu_custom_call" | custom-call | tf_op jit(solution)/shard_map/pallas_call | solution.py:404
